TPU v7x, 512 devices: a 8x2x16 block of a 8x8x16 slice. The times are simulated.
512 devices in a mesh: ga: 2 (over y), gx: 16 (over z), gy: 8 (over x), col: 2 (over core).
Axes of the slice: x: 8, y: 2, z: 16, core: 2. Of those that a mesh axis runs over, the one named last changes fastest.
The devices are a block of a 8x8x16 slice.
Arguments:
- pair_rep: bfloat16 [2, 640, 640, 128], P('ga', 'gx', 'gy'), parts along dimension 0, may hold values from -6 to 6
- pair_mask: int32 [2, 640, 640], P('ga', 'gx', 'gy'), parts along dimension 0, may hold values 0 or 1
- amax_history: float32 [2, 128], P(None, 'col'), may hold values from 0.3 to 3
- in_gain: float32 [128], replicated, may hold values from 0.5 to 1.5
- in_bias: float32 [128], replicated, may hold values from -3 to 3
- proj_weight: bfloat16 [128, 4, 128], P(None, None, 'col'), may hold values from -0.5 to 0.5
- gate_weight: bfloat16 [128, 128], P(None, 'col'), may hold values from -0.5 to 0.5
- out_gain: float32 [128], replicated, may hold values from 0.5 to 1.5
- out_bias: float32 [128], replicated, may hold values from -3 to 3
- out_weight: bfloat16 [128, 128], P(None, 'col'), may hold values from -0.5 to 0.5
Outputs:
- update: bfloat16 [2, 640, 640, 128], P('ga', 'gx', 'gy', 'col'), parts along dimension 0
- new_amax: float32 [4, 128], P('ga', 'col'), parts along dimension 0
There are 2 independent parts, one for each index of `ga`. A program takes and returns all parts, laid end to end along the dimension named above; an argument that names none is the same for every part. Nothing has to cross between parts.
All inputs are finite; a program needn't handle non-finite values. No bound on the sum of `pair_mask` on one device may be relied on, other than what follows from the above.
Results may differ from a plain program's by a relative error of at most 0.0065.
Values may be sent and summed in bfloat16 or wider, within the bound.
No kernel may reach another device: no remote copies, remote signals or barrier semaphores. Data moves between devices by JAX's collectives and lax.ppermute only.
A program may use at most 128 MiB of HBM per device.

v0:
```python
import jax
import jax.numpy as jnp
from jax import lax
from jax.sharding import PartitionSpec as P

epsilon = 1e-05
format_limit = 448.0


def broadcast(block, axis, holder):
    block = jnp.where(lax.axis_index(axis) == holder, block, jnp.zeros_like(block))
    return lax.psum(block, axis)


def copy_for_each(array, axis):
    copies = jnp.broadcast_to(array, (lax.axis_size(axis), *array.shape))
    return lax.all_to_all(copies, axis, split_axis=0, concat_axis=0, tiled=True)


def joined_along(parts, dim):
    dims = list(parts.shape[1:])
    dims[dim] *= parts.shape[0]
    return jnp.moveaxis(parts, 0, dim).reshape(dims)


def gather_directly(array, axis, dim):
    parts = copy_for_each(array, axis)
    return joined_along(parts, dim)


def total_of_pieces(array, axis):
    parts = lax.all_gather(array, axis)
    return parts.max(axis=0)


def layer_norm(values, gain, bias):
    average = jnp.mean(values, axis=-1, keepdims=True)
    spread = jnp.mean(jnp.square(values - average), axis=-1, keepdims=True)
    return (values - average) * lax.rsqrt(spread + epsilon) * gain + bias


def crop_triangle(left_q, right_q):
    wide_rows = lax.all_gather(right_q, "gy", axis=2, tiled=True)
    row_ratio = lax.axis_size("gx") // lax.axis_size("gy")
    first_root = lax.axis_index("gy") * row_ratio
    received = [
        broadcast(wide_rows, "gx", first_root + offset_step) for offset_step in range(row_ratio)
    ]
    panel = jnp.concatenate(received, axis=1)
    return jnp.einsum(
        "cik,cjk->cij", gather_directly(left_q, "gy", 2), panel, preferred_element_type=jnp.float32
    )


def on_device(
    pair_rep,
    pair_mask,
    amax_history,
    in_gain,
    in_bias,
    proj_weight,
    gate_weight,
    out_gain,
    out_bias,
    out_weight,
):
    normed = layer_norm(pair_rep.astype(jnp.float32), in_gain, in_bias).astype(jnp.bfloat16)
    projected = jnp.einsum(
        "bikd,dsc->scbik", normed, proj_weight, preferred_element_type=jnp.float32
    )
    masking = pair_mask.astype(jnp.float32)[None]
    left_proj = masking * jax.nn.sigmoid(projected[1]) * projected[0]
    right_proj = masking * jax.nn.sigmoid(projected[3]) * projected[2]
    local_max = jnp.stack(
        [jnp.max(jnp.abs(left_proj), axis=(1, 2, 3)), jnp.max(jnp.abs(right_proj), axis=(1, 2, 3))]
    )
    new_amax = total_of_pieces(local_max, ("gx", "gy"))
    scales = amax_history / format_limit
    left_q = jnp.clip(
        left_proj / scales[0][:, None, None, None], -format_limit, format_limit
    ).astype(jnp.bfloat16)
    right_q = jnp.clip(
        right_proj / scales[1][:, None, None, None], -format_limit, format_limit
    ).astype(jnp.bfloat16)
    products = jnp.stack([crop_triangle(left_q[:, 0], right_q[:, 0])], axis=1)
    triangle = (products * (scales[0] * scales[1])[:, None, None, None]).astype(jnp.bfloat16)
    gathered = lax.all_gather(triangle, "col", axis=0, tiled=True).astype(jnp.float32)
    average = jnp.mean(gathered, axis=0, keepdims=True)
    spread = jnp.mean(jnp.square(gathered - average), axis=0, keepdims=True)
    tnorm = (
        (gathered - average) * lax.rsqrt(spread + epsilon) * out_gain[:, None, None, None]
        + out_bias[:, None, None, None]
    ).astype(jnp.bfloat16)
    mixing = jnp.einsum("cbij,cd->bijd", tnorm, out_weight, preferred_element_type=jnp.float32)
    gating = jax.nn.sigmoid(
        jnp.einsum("bijd,dc->bijc", normed, gate_weight, preferred_element_type=jnp.float32)
    )
    update = (gating * mixing).astype(jnp.bfloat16)
    return (update, new_amax)


def solution(mesh):
    placed = (
        P("ga", "gx", "gy", None),
        P("ga", "gx", "gy"),
        P(None, "col"),
        P(),
        P(),
        P(None, None, "col"),
        P(None, "col"),
        P(),
        P(),
        P(None, "col"),
    )
    return jax.shard_map(
        on_device,
        mesh=mesh,
        in_specs=placed,
        out_specs=(P("ga", "gx", "gy", "col"), P("ga", "col")),
        check_vma=False,
    )
```

profile of v0, /device:TPU:65, one launch (start us, length us, event | category | flops | bytes accessed | tf_op | source)
XLA Modules:
  0.0 403.0 jit_solution(6059494972928307105)
XLA Ops:
  7.2 0.1 all-gather.5.cloned.1.call-start
  7.3 0.7 broadcast_multiply_fusion.2
  8.0 0.7 convert_bitcast_fusion.1
  8.8 1.6 convert_reduce_fusion.1
  10.4 2.3 fusion.13
  12.8 2.1 convolution_bitcast_fusion
  14.9 2.3 fusion.45
  17.1 0.2 copy-done.1
  17.4 1.3 copy.23
  18.7 0.1 all-gather.5.cloned.1.call-update
  18.8 0.1 all-reduce.3.cloned.1.call-start
  18.8 117.4 %all-gather.5.cloned.1.call-done = bf16[64,40,640]{0,1,2:T(8,128)(2,1)} async-done(((bf16[64,40,80]{0,1,2:T(8,128)(2,1)}), bf16[64,40,640]{0,1,2:T(8,128)(2,1)}) %all-gather.5.cloned.1.call-update) | async-done | bytes 3276816 | tf_op jit(solution)/shard_map/all_gather | solution.py:43
  136.3 14.6 %copy.24 = bf16[64,40,640]{2,1,0:T(8,128)(2,1)S(1)} copy(bf16[64,40,640]{0,1,2:T(8,128)(2,1)} %all-gather.5.cloned.1.call-done) | data formatting | bytes 6553600 | tf_op jit(solution)/shard_map/all_gather | solution.py:43
  150.8 3.3 broadcast_select_fusion.1
  154.1 0.1 all-reduce.3.cloned.1.call-update
  154.2 1.0 copy-done.4
  155.2 0.4 copy.20
  155.6 3.0 broadcast_in_dim.2
  158.6 4.8 %all-to-all-start = ((bf16[8,64,40,80]{3,2,1,0:T(8,128)(2,1)}), bf16[8,64,40,80]{3,2,1,0:T(8,128)(2,1)}, u32[]{:S(2)}, u32[]{:S(2)}) async-start(bf16[8,64,40,80]{3,2,1,0:T(8,128)(2,1)} %broadcast_in_dim.2), calls=%async_computation | async-start | bytes 10485760 | tf_op jit(solution)/shard_map/all_to_all | solution.py:17
  163.5 3.5 fusion.37
  167.0 185.1 %all-gather.2 = f32[128,2,64]{2,1,0:T(2,128)S(1)} all-gather(f32[1,2,64]{2,1,0:T(2,128)S(1)} %maximum_bitcast_fusion), channel_id=3, replica_groups=mesh['ga'=2,'gx'=16,'gy'=8,'col'=2] {'gx','gy'}, dimensions={0}, use_global_device_ids=true | all-gather | bytes 66048 | tf_op jit(solution)/shard_map/all_gather | solution.py:32
  352.2 0.7 reduce_max.29
  352.9 2.3 fusion.19
  355.2 10.9 %copy.21 = bf16[64,40,8,80]{3,2,1,0:T(8,128)(2,1)} copy(bf16[64,40,8,80]{3,1,0,2:T(8,128)(2,1)} %bitcast.10) | data formatting | bytes 6553600 | tf_op jit(solution)/shard_map/transpose | solution.py:23
  366.1 7.2 %reshape.236 = bf16[64,40,640]{2,1,0:T(8,128)(2,1)S(1)} reshape(bf16[64,40,8,80]{3,2,1,0:T(8,128)(2,1)} %copy.21) | data formatting | bytes 6553600 | tf_op jit(solution)/shard_map/reshape | solution.py:23
  373.3 5.1 %fusion.23 = bf16[64,40,80]{2,1,0:T(8,128)(2,1)S(1)} fusion(bf16[64,40,640]{2,1,0:T(8,128)(2,1)S(1)} %reshape.236, bf16[64,40,640]{2,1,0:T(8,128)(2,1)} %get-tuple-element.4, bf16[64,40,640]{2,1,0:T(8,128)(2,1)} %get-tuple-element.5, f32[64]{0:T(128)S(1)} %fusion.58), kind=kOutput, calls=%fused_computation.30 | convolution fusion | flops 275660800 | bytes 10240256 | tf_op jit(solution)/shard_map/cik,cjk->cij/dot_general | solution.py:50
  378.4 14.5 %all-gather = bf16[128,40,80]{2,1,0:T(8,128)(2,1)S(1)} all-gather(bf16[64,40,80]{2,1,0:T(8,128)(2,1)S(1)} %fusion.23), channel_id=2, replica_groups=mesh['ga'=2,'gx'=16,'gy'=8,'col'=2] {'col'}, dimensions={0}, use_global_device_ids=true | all-gather | bytes 1228800 | tf_op jit(solution)/shard_map/all_gather | solution.py:87
  392.9 0.3 convert_reduce_fusion
  393.2 0.5 fusion.7
  393.7 0.5 fusion.27
  394.3 0.7 copy-done.5
  395.0 1.2 fusion.47
  (30 shorter events, 0.1 us)
Async XLA Ops:
  7.2 5.5 %copy-start = (bf16[128,4,64]{0,2,1:T(8,128)(2,1)S(1)}, bf16[128,4,64]{0,2,1:T(8,128)(2,1)}, u32[]{:S(2)}) copy-start(bf16[128,4,64]{0,2,1:T(8,128)(2,1)} %param.15) | copy-start | bytes 196612
  7.2 5.5 %copy-start.2 = (bf16[1,40,80,128]{3,2,1,0:T(8,128)(2,1)S(1)}, bf16[1,40,80,128]{3,2,1,0:T(8,128)(2,1)}, u32[]{:S(2)}) copy-start(bf16[1,40,80,128]{3,2,1,0:T(8,128)(2,1)} %param.10) | copy-start | bytes 2457604
  7.2 5.5 %copy-start.7 = (f32[128]{0:T(128)S(1)}, f32[128]{0:T(128)}, u32[]{:S(2)}) copy-start(f32[128]{0:T(128)} %param.14) | copy-start | bytes 1540
  7.2 5.5 %copy-start.8 = (f32[128]{0:T(128)S(1)}, f32[128]{0:T(128)}, u32[]{:S(2)}) copy-start(f32[128]{0:T(128)} %param.13) | copy-start | bytes 1540
  7.2 129.0 %all-gather.5.cloned.1.call-start = ((), (), s32[]{:S(2)}) async-start(), calls=%async_computation.1 | async-start | bytes 7372800 | tf_op jit(solution)/shard_map/all_gather | solution.py:43
  14.9 2.5 copy-start.1
  18.8 354.5 %all-reduce.3.cloned.1.call-start = ((), (), s32[]{:S(2)}) async-start(), calls=%async_computation.2 | async-start | bytes 13107200 | tf_op jit(solution)/shard_map/psum | solution.py:12
  154.1 1.1 copy-start.4
  158.6 196.6 %all-to-all-start = ((bf16[8,64,40,80]{3,2,1,0:T(8,128)(2,1)}), bf16[8,64,40,80]{3,2,1,0:T(8,128)(2,1)}, u32[]{:S(2)}, u32[]{:S(2)}) async-start(bf16[8,64,40,80]{3,2,1,0:T(8,128)(2,1)} %broadcast_in_dim.2), calls=%async_computation | async-start | bytes 10485760 | tf_op jit(solution)/shard_map/all_to_all | solution.py:17
  163.5 189.4 %copy-start.3 = (bf16[1,40,80,128]{3,2,1,0:T(8,128)(2,1)S(1)}, bf16[1,40,80,128]{3,2,1,0:T(8,128)(2,1)}, u32[]{:S(2)}) copy-start(bf16[1,40,80,128]{3,2,1,0:T(8,128)(2,1)} %param.10) | copy-start | bytes 2457604
  163.5 189.4 %copy-start.11 = (bf16[128,64]{0,1:T(8,128)(2,1)S(1)}, bf16[128,64]{0,1:T(8,128)(2,1)}, u32[]{:S(2)}) copy-start(bf16[128,64]{0,1:T(8,128)(2,1)} %param.16) | copy-start | bytes 49156
  392.9 0.8 copy-start.9
  392.9 0.8 copy-start.10
  393.7 1.3 copy-start.5
  393.7 1.3 copy-start.6
Sparse Core Ops, SparseCore 0:
  18.9 117.3 all-gather.4
  154.3 179.9 all-reduce.2
where the time goes:
time: 404 us; the launch traced here: 403 us
  blocking collectives  200 us (50%)
  waiting for transfers between devices  118 us (29%)
  local copies, waits for them, and re-layouts  39.4 us (10%)
  other arithmetic  16.5 us (4%)
  between operations  14.3 us (4%)
  matrix products  10.7 us (3%)
  starting transfers between devices  4.97 us (1%)
    all_gather x1, blocking collectives, total_of_pieces(): parts = lax.all_gather(array, axis)  185 us
    all_gather x1, waiting for transfers between devices, crop_triangle(): wide_rows = lax.all_gather(right_q, 'gy', axis=2, tiled=True)  117 us
    all_gather x1, local copies, waits for them, and re-layouts, crop_triangle(): wide_rows = lax.all_gather(right_q, 'gy', axis=2, tiled=True)  14.6 us
    all_gather x1, blocking collectives, on_device(): lax.all_gather(triangle, 'col', axis=0, tiled=True).astype(jnp.float32)  14.5 us
    transpose x1, local copies, waits for them, and re-layouts, joined_along(): return jnp.moveaxis(parts, 0, dim).reshape(dims)  10.9 us
  transfers between devices with their start and end apart: 3, of which 1 were waited for; matrix products, arithmetic and copies ran while one was open for 7% of the time, Pallas kernels for 0%

commit v1 on v0

--- a/solution.py
+++ b/solution.py
@@ -40,7 +40,8 @@
 
 
 def crop_triangle(left_q, right_q):
-    wide_rows = lax.all_gather(right_q, "gy", axis=2, tiled=True)
+    copies_2 = jnp.concatenate([right_q] * lax.axis_size("gy"), axis=2)
+    wide_rows = lax.all_to_all(copies_2, "gy", 2, 2, tiled=True)
     row_ratio = lax.axis_size("gx") // lax.axis_size("gy")
     first_root = lax.axis_index("gy") * row_ratio
     received = [

time: 404 us -> 440 us (1.089)
  waiting for transfers between devices: 118 us -> 41.9 us
  blocking collectives: 200 us -> 271 us
  local copies, waits for them, and re-layouts: 39.4 us -> 72.1 us
  starting transfers between devices: 4.97 us -> 12.8 us
    all_gather x1 -> x0, waiting for transfers between devices: 117 us -> none  [crop_triangle(): wide_rows = lax.all_gather(right_q, 'gy', axis=2, tiled=True)]
    all_gather x1, blocking collectives: 185 us -> 255 us  [total_of_pieces(): parts = lax.all_gather(array, axis)]
    all_to_all x0 -> x1, waiting for transfers between devices: none -> 41.8 us  [crop_triangle(): wide_rows = lax.all_to_all(copies_2, 'gy', 2, 2, tiled=True)]
    concatenate x0 -> x2, local copies, waits for them, and re-layouts: none -> 18.5 us  [crop_triangle(): copies_2 = jnp.concatenate([right_q] * lax.axis_size('gy'), axis=2)]
    unnamed x24 -> x28, local copies, waits for them, and re-layouts: 2.02 us -> 17.5 us
    all_gather x1 -> x0, local copies, waits for them, and re-layouts: 14.6 us -> none  [crop_triangle(): wide_rows = lax.all_gather(right_q, 'gy', axis=2, tiled=True)]
    all_to_all x0 -> x1, local copies, waits for them, and re-layouts: none -> 14.6 us  [crop_triangle(): wide_rows = lax.all_to_all(copies_2, 'gy', 2, 2, tiled=True)]
    all_to_all x0 -> x1, starting transfers between devices: none -> 7.85 us  [crop_triangle(): wide_rows = lax.all_to_all(copies_2, 'gy', 2, 2, tiled=True)]
  transfers between devices with their start and end apart: 3 -> 3, of which waited for: 1 -> 1; matrix products, arithmetic and copies ran while one was open for 7% -> 6% of each run, Pallas kernels for 0% -> 0%
where the time goes in v1:
time: 440 us; the launch traced here: 439 us
  blocking collectives  271 us (62%)
  local copies, waits for them, and re-layouts  72.1 us (16%)
  waiting for transfers between devices  41.9 us (10%)
  other arithmetic  16.6 us (4%)
  between operations  14.3 us (3%)
  starting transfers between devices  12.8 us (3%)
  matrix products  10.7 us (2%)
    all_gather x1, blocking collectives, total_of_pieces(): parts = lax.all_gather(array, axis)  255 us
    all_to_all x1, waiting for transfers between devices, crop_triangle(): wide_rows = lax.all_to_all(copies_2, 'gy', 2, 2, tiled=True)  41.8 us
    concatenate x2, local copies, waits for them, and re-layouts, crop_triangle(): copies_2 = jnp.concatenate([right_q] * lax.axis_size('gy'), axis=2)  18.5 us
    unnamed x28, local copies, waits for them, and re-layouts  17.5 us
    all_gather x1, blocking collectives, on_device(): lax.all_gather(triangle, 'col', axis=0, tiled=True).astype(jnp.float32)  16.5 us
    all_to_all x1, local copies, waits for them, and re-layouts, crop_triangle(): wide_rows = lax.all_to_all(copies_2, 'gy', 2, 2, tiled=True)  14.6 us
    transpose x1, local copies, waits for them, and re-layouts, joined_along(): return jnp.moveaxis(parts, 0, dim).reshape(dims)  10.9 us
  transfers between devices with their start and end apart: 3, of which 1 were waited for; matrix products, arithmetic and copies ran while one was open for 6% of the time, Pallas kernels for 0%

profile of v1, /device:TPU:65, one launch (start us, length us, event | category | flops | bytes accessed | tf_op | source)
XLA Modules:
  0.0 439.4 jit_solution(13797238662879740413)
XLA Ops:
  7.2 0.8 broadcast_multiply_fusion.2
  8.0 0.7 convert_bitcast_fusion.1
  8.7 1.6 convert_reduce_fusion.1
  10.3 2.3 fusion.13
  12.7 2.1 convolution_bitcast_fusion
  14.8 2.3 fusion.45
  17.1 0.2 copy-done.2
  17.4 7.5 %concatenate.6 = bf16[64,40,640]{2,0,1:T(8,128)(2,1)} concatenate(bf16[64,40,80]{2,0,1:T(8,128)(2,1)S(1)} %get-tuple-element.6, bf16[64,40,80]{2,0,1:T(8,128)(2,1)S(1)} %get-tuple-element.6, bf16[64,40,80]{2,0,1:T(8,128)(2,1)S(1)} %get-tuple-element.6, bf16[64,40,80]{2,0,1:T(8,128)(2,1)S(1)} %get-tuple-element.6, bf16[64,40,80]{2,0,1:T(8,128)(2,1)S(1)} %get-tuple-element.6, ...), dimensions={2} | concatenate | bytes 6553600 | tf_op jit(solution)/shard_map/concatenate | solution.py:43
  24.8 11.0 %copy.23 = bf16[64,40,640]{0,1,2:T(8,128)(2,1)} copy(bf16[64,40,640]{2,0,1:T(8,128)(2,1)} %concatenate.6) | data formatting | bytes 6553600 | tf_op jit(solution)/shard_map/concatenate | solution.py:43
  35.9 9.1 %reshape.248 = bf16[8,2,102400]{2,1,0:T(2,128)(2,1)} reshape(bf16[640,40,64]{2,1,0:T(8,128)(2,1)} %bitcast.136) | data formatting | bytes 6553600
  45.0 7.9 %all-to-all-start.1 = ((bf16[8,2,102400]{2,1,0:T(2,128)(2,1)}), bf16[8,2,102400]{2,1,0:T(2,128)(2,1)S(1)}, u32[]{:S(2)}, u32[]{:S(2)}) async-start(bf16[8,2,102400]{2,1,0:T(2,128)(2,1)} %reshape.248), calls=%async_computation.1 | async-start | bytes 6553600 | tf_op jit(solution)/shard_map/all_to_all | solution.py:44
  52.9 41.8 %all-to-all-done.1 = bf16[8,2,102400]{2,1,0:T(2,128)(2,1)S(1)} async-done(((bf16[8,2,102400]{2,1,0:T(2,128)(2,1)}), bf16[8,2,102400]{2,1,0:T(2,128)(2,1)S(1)}, u32[]{:S(2)}, u32[]{:S(2)}) %all-to-all-start.1) | async-done | bytes 3276832 | tf_op jit(solution)/shard_map/all_to_all | solution.py:44
  94.7 6.4 %reshape.249 = bf16[640,40,64]{2,1,0:T(8,128)(2,1)} reshape(bf16[8,2,102400]{2,1,0:T(2,128)(2,1)S(1)} %all-to-all-done.1) | data formatting | bytes 6553600
  101.1 14.6 %copy.24 = bf16[64,40,640]{2,1,0:T(8,128)(2,1)S(1)} copy(bf16[64,40,640]{0,1,2:T(8,128)(2,1)} %bitcast.137) | data formatting | bytes 6553600 | tf_op jit(solution)/shard_map/all_to_all | solution.py:44
  115.6 3.3 broadcast_select_fusion.1
  119.0 1.0 copy-done.5
  120.1 0.4 copy.20
  120.5 3.0 broadcast_in_dim.2
  123.5 4.8 %all-to-all-start = ((bf16[8,64,40,80]{3,2,1,0:T(8,128)(2,1)}), bf16[8,64,40,80]{3,2,1,0:T(8,128)(2,1)}, u32[]{:S(2)}, u32[]{:S(2)}) async-start(bf16[8,64,40,80]{3,2,1,0:T(8,128)(2,1)} %broadcast_in_dim.2), calls=%async_computation | async-start | bytes 10485760 | tf_op jit(solution)/shard_map/all_to_all | solution.py:17
  128.4 3.5 fusion.37
  131.9 254.6 %all-gather.2 = f32[128,2,64]{2,1,0:T(2,128)S(1)} all-gather(f32[1,2,64]{2,1,0:T(2,128)S(1)} %maximum_bitcast_fusion), channel_id=3, replica_groups=mesh['ga'=2,'gx'=16,'gy'=8,'col'=2] {'gx','gy'}, dimensions={0}, use_global_device_ids=true | all-gather | bytes 66048 | tf_op jit(solution)/shard_map/all_gather | solution.py:32
  386.5 0.7 reduce_max.29
  387.2 2.3 fusion.19
  389.6 10.9 %copy.21 = bf16[64,40,8,80]{3,2,1,0:T(8,128)(2,1)} copy(bf16[64,40,8,80]{3,1,0,2:T(8,128)(2,1)} %bitcast.10) | data formatting | bytes 6553600 | tf_op jit(solution)/shard_map/transpose | solution.py:23
  400.4 7.2 %reshape.236 = bf16[64,40,640]{2,1,0:T(8,128)(2,1)S(1)} reshape(bf16[64,40,8,80]{3,2,1,0:T(8,128)(2,1)} %copy.21) | data formatting | bytes 6553600 | tf_op jit(solution)/shard_map/reshape | solution.py:23
  407.6 5.1 %fusion.23 = bf16[64,40,80]{2,1,0:T(8,128)(2,1)S(1)} fusion(bf16[64,40,640]{2,1,0:T(8,128)(2,1)S(1)} %reshape.236, bf16[64,40,640]{2,1,0:T(8,128)(2,1)} %get-tuple-element.4, bf16[64,40,640]{2,1,0:T(8,128)(2,1)} %get-tuple-element.5, f32[64]{0:T(128)S(1)} %fusion.58), kind=kOutput, calls=%fused_computation.30 | convolution fusion | flops 275660800 | bytes 10240256 | tf_op jit(solution)/shard_map/cik,cjk->cij/dot_general | solution.py:51
  412.8 16.5 %all-gather = bf16[128,40,80]{2,1,0:T(8,128)(2,1)S(1)} all-gather(bf16[64,40,80]{2,1,0:T(8,128)(2,1)S(1)} %fusion.23), channel_id=2, replica_groups=mesh['ga'=2,'gx'=16,'gy'=8,'col'=2] {'col'}, dimensions={0}, use_global_device_ids=true | all-gather | bytes 1228800 | tf_op jit(solution)/shard_map/all_gather | solution.py:88
  429.3 0.3 convert_reduce_fusion
  429.6 0.5 fusion.7
  430.1 0.5 fusion.27
  430.7 0.7 copy-done.6
  431.4 1.2 fusion.47
  (34 shorter events, 0.3 us)
Async XLA Ops:
  7.2 5.5 %copy-start = (bf16[128,4,64]{0,2,1:T(8,128)(2,1)S(1)}, bf16[128,4,64]{0,2,1:T(8,128)(2,1)}, u32[]{:S(2)}) copy-start(bf16[128,4,64]{0,2,1:T(8,128)(2,1)} %param.15) | copy-start | bytes 196612
  7.2 5.5 %copy-start.3 = (bf16[1,40,80,128]{3,2,1,0:T(8,128)(2,1)S(1)}, bf16[1,40,80,128]{3,2,1,0:T(8,128)(2,1)}, u32[]{:S(2)}) copy-start(bf16[1,40,80,128]{3,2,1,0:T(8,128)(2,1)} %param.10) | copy-start | bytes 2457604
  7.2 5.5 %copy-start.8 = (f32[128]{0:T(128)S(1)}, f32[128]{0:T(128)}, u32[]{:S(2)}) copy-start(f32[128]{0:T(128)} %param.14) | copy-start | bytes 1540
  7.2 5.5 %copy-start.9 = (f32[128]{0:T(128)S(1)}, f32[128]{0:T(128)}, u32[]{:S(2)}) copy-start(f32[128]{0:T(128)} %param.13) | copy-start | bytes 1540
  14.8 2.6 copy-start.2
  45.0 49.7 %all-to-all-start.1 = ((bf16[8,2,102400]{2,1,0:T(2,128)(2,1)}), bf16[8,2,102400]{2,1,0:T(2,128)(2,1)S(1)}, u32[]{:S(2)}, u32[]{:S(2)}) async-start(bf16[8,2,102400]{2,1,0:T(2,128)(2,1)} %reshape.248), calls=%async_computation.1 | async-start | bytes 6553600 | tf_op jit(solution)/shard_map/all_to_all | solution.py:44
  52.8 354.8 %all-reduce.3.cloned.1.call-start = ((), (), s32[]{:S(2)}) async-start(), calls=%async_computation.2 | async-start | bytes 13107200 | tf_op jit(solution)/shard_map/psum | solution.py:12
  119.0 1.1 copy-start.5
  123.5 266.1 %all-to-all-start = ((bf16[8,64,40,80]{3,2,1,0:T(8,128)(2,1)}), bf16[8,64,40,80]{3,2,1,0:T(8,128)(2,1)}, u32[]{:S(2)}, u32[]{:S(2)}) async-start(bf16[8,64,40,80]{3,2,1,0:T(8,128)(2,1)} %broadcast_in_dim.2), calls=%async_computation | async-start | bytes 10485760 | tf_op jit(solution)/shard_map/all_to_all | solution.py:17
  128.3 258.9 %copy-start.4 = (bf16[1,40,80,128]{3,2,1,0:T(8,128)(2,1)S(1)}, bf16[1,40,80,128]{3,2,1,0:T(8,128)(2,1)}, u32[]{:S(2)}) copy-start(bf16[1,40,80,128]{3,2,1,0:T(8,128)(2,1)} %param.10) | copy-start | bytes 2457604
  128.4 258.9 %copy-start.12 = (bf16[128,64]{0,1:T(8,128)(2,1)S(1)}, bf16[128,64]{0,1:T(8,128)(2,1)}, u32[]{:S(2)}) copy-start(bf16[128,64]{0,1:T(8,128)(2,1)} %param.16) | copy-start | bytes 49156
  429.2 0.8 copy-start.10
  429.3 0.8 copy-start.11
  430.0 1.3 copy-start.6
  430.0 1.3 copy-start.7
  430.1 2.4 copy-start.1
Sparse Core Ops, SparseCore 0:
  119.2 243.7 all-reduce.2
